TPU v7x, 32 devices: a whole 2x2x4 slice. The times are simulated.
32 devices in a mesh: head: 4 (over x, core), ctx: 8 (over z, y).
Axes of the slice: x: 2, y: 2, z: 4, core: 2. Of those that a mesh axis runs over, the one named last changes fastest.
Arguments:
- query: bfloat16 [2048, 16384], P(('head', 'ctx')), may hold values from -5 to 5
- key: bfloat16 [2048, 1024], P(('head', 'ctx')), may hold values from -5 to 5
- value: bfloat16 [2048, 1024], P(('head', 'ctx')), may hold values from -6 to 6
- block_order: int32 [32], replicated, may hold values from 0 to 31, each once
Outputs:
- attended: bfloat16 [2048, 16384], P(('head', 'ctx'))
- log_norm_rows: float32 [2048, 128], P(('head', 'ctx'))
All inputs are finite; a program needn't handle non-finite values.
Results may differ from a plain program's by a relative error of at most 0.0036.
Values may be sent and summed in bfloat16 or wider, within the bound.
A program may use at most 64 MiB of HBM per device.

v0:
```python
import math

import jax
import jax.numpy as jnp
from jax import lax
from jax.sharding import PartitionSpec as P

HEAD_DIMENSION = 128


def passed_along(block, axis, distance):
    devices = range(lax.axis_size(axis))
    route = [((i - distance) % len(devices), i) for i in devices]
    return lax.ppermute(block, axis, route)


def partial_terms(queries, keys, values, query_positions, key_pos):
    rows = queries.shape[0]
    kv_heads = keys.shape[1] // HEAD_DIMENSION
    width = queries.shape[1] // kv_heads
    group = width // HEAD_DIMENSION
    scale = 1.0 / math.sqrt(HEAD_DIMENSION)
    visible = key_pos[None, :] <= query_positions[:, None]
    peaks = []
    totals = []
    accs = []
    for head in range(kv_heads):
        q_head = queries[:, head * width : (head + 1) * width].reshape(rows, group, HEAD_DIMENSION)
        key_head_index = keys[:, head * HEAD_DIMENSION : (head + 1) * HEAD_DIMENSION]
        v_head = values[:, head * HEAD_DIMENSION : (head + 1) * HEAD_DIMENSION]
        score_matrix = (
            jnp.einsum("rgd,kd->grk", q_head, key_head_index, preferred_element_type=jnp.float32)
            * scale
        )
        shifted = jnp.where(visible[None], score_matrix, -1e30)
        peak = jnp.maximum(jnp.max(shifted, axis=-1), -10000.0)
        weights = jnp.exp(shifted - peak[..., None])
        total = jnp.sum(weights, axis=-1)
        probs = weights.astype(jnp.bfloat16)
        acc = jnp.einsum("grk,kd->rgd", probs, v_head, preferred_element_type=jnp.float32)
        peaks.append(peak.T)
        totals.append(total.T)
        accs.append(acc.reshape(rows, width))
    return (
        jnp.concatenate(peaks, axis=1),
        jnp.concatenate(totals, axis=1),
        jnp.concatenate(accs, axis=1),
    )


def combine(first, second):
    peak_a, total_a, acc_a = first
    peak_b, total_b, acc_b = second
    peak = jnp.maximum(peak_a, peak_b)
    factor_a = jnp.exp(peak_a - peak)
    factor_b = jnp.exp(peak_b - peak)
    total = total_a * factor_a + total_b * factor_b
    rows, heads = peak.shape
    acc = (
        acc_a.reshape(rows, heads, -1) * factor_a[..., None]
        + acc_b.reshape(rows, heads, -1) * factor_b[..., None]
    )
    result = (acc / total[..., None]).reshape(rows, -1)
    return (result, peak + jnp.log(total))


def body(query, key, value, block_order):
    n_head = lax.axis_size("head")
    n_ctx = lax.axis_size("ctx")
    block = query.shape[0]
    here_head = lax.axis_index("head")
    here_ctx = lax.axis_index("ctx")
    offsets = jnp.arange(block, dtype=jnp.int32)

    def shard_positions(shard):
        stored = jnp.arange(n_head, dtype=jnp.int32) * n_ctx + shard
        starts = block_order[stored] * block
        return (starts[:, None] + offsets[None, :]).reshape(-1)

    before = (here_ctx - 1) % n_ctx
    local_positions = shard_positions(here_ctx)
    prev_pos = shard_positions(before)
    keys_all, values_all = (
        lax.all_gather(key, "head", axis=0, tiled=True),
        lax.all_gather(value, "head", axis=0, tiled=True),
    )
    keys_prev, values_prev = passed_along((keys_all, values_all), "ctx", 1)
    query_positions = block_order[here_head * n_ctx + here_ctx] * block + offsets
    own = partial_terms(query, keys_all, values_all, query_positions, local_positions)
    far = partial_terms(query, keys_prev, values_prev, query_positions, prev_pos)
    result, lse = combine(own, far)
    return (result.astype(jnp.bfloat16), lse)


def solution(mesh):
    placed = (P(("head", "ctx"), None), P(("head", "ctx"), None), P(("head", "ctx"), None), P())
    return jax.shard_map(
        body,
        mesh=mesh,
        in_specs=placed,
        out_specs=(P(("head", "ctx"), None), P(("head", "ctx"), None)),
        check_vma=False,
    )
```

profile of v0, /device:TPU:0, one launch (start us, length us, event | category | flops | bytes accessed | tf_op | source)
XLA Modules:
  0.0 79.2 jit_solution(3487028568458188250)
XLA Ops:
  0.6 10.2 %all_gather.7 = bf16[256,1024]{1,0:T(8,128)(2,1)} all-gather(bf16[64,1024]{1,0:T(8,128)(2,1)} %param.6), channel_id=1, replica_groups=mesh['head'=4,'ctx'=8] {'head'}, dimensions={0}, use_global_device_ids=true | all-gather | bytes 655360 | tf_op jit(solution)/shard_map/all_gather | solution.py:85
  10.8 1.5 %collective-permute-start.1 = (bf16[256,1024]{1,0:T(8,128)(2,1)}, bf16[256,1024]{1,0:T(8,128)(2,1)}, u32[]{:S(2)}, u32[]{:S(2)}) collective-permute-start(bf16[256,1024]{1,0:T(8,128)(2,1)} %all_gather.7), channel_id=1, source_target_pairs={{7,0},{0,1},{1,2},{2,3},{3,4},{4,5},{5,6},{6,7},{15,8},{8,9},{9,10... | collective-permute-start | bytes 1572872 | tf_op jit(solution)/shard_map/ppermute | solution.py:14
  12.4 7.2 %all_gather.6 = bf16[256,1024]{1,0:T(8,128)(2,1)S(1)} all-gather(bf16[64,1024]{1,0:T(8,128)(2,1)} %param.5), channel_id=1, replica_groups=mesh['head'=4,'ctx'=8] {'head'}, dimensions={0}, use_global_device_ids=true | all-gather | bytes 655360 | tf_op jit(solution)/shard_map/all_gather | solution.py:84
  19.6 1.5 %collective-permute-start = (bf16[256,1024]{1,0:T(8,128)(2,1)S(1)}, bf16[256,1024]{1,0:T(8,128)(2,1)S(1)}, u32[]{:S(2)}, u32[]{:S(2)}) collective-permute-start(bf16[256,1024]{1,0:T(8,128)(2,1)S(1)} %all_gather.6), channel_id=1, source_target_pairs={{7,0},{0,1},{1,2},{2,3},{3,4},{4,5},{5,6},{6,7},{15,8},{8,9},{9,10... | collective-permute-start | bytes 1572872 | tf_op jit(solution)/shard_map/ppermute | solution.py:14
  21.1 1.2 %dynamic_slice.3 = s32[1]{0:T(128)} dynamic-slice(s32[32]{0:T(128)} %param.7, s32[]{:T(128)S(6)} %select_n.80), dynamic_slice_sizes={1} | dynamic-slice | bytes 12 | tf_op jit(solution)/shard_map/dynamic_slice | solution.py:88
  23.0 1.3 %gather_fusion.1 = s32[4]{0:T(128)S(1)} fusion(s32[32]{0:T(128)} %param.7, s32[1024]{0:T(1024)S(1)} %get-tuple-element.50), kind=kCustom, calls=%fused_computation.1 | custom fusion | bytes 48 | tf_op jit(solution)/shard_map/gather | solution.py:77
  24.3 1.3 %gather_fusion = s32[4]{0:T(128)S(1)} fusion(s32[32]{0:T(128)} %param.7, s32[1024]{0:T(1024)S(1)} %get-tuple-element.51), kind=kCustom, calls=%fused_computation | custom fusion | bytes 48 | tf_op jit(solution)/shard_map/gather | solution.py:77
  25.9 1.6 %slice_bitcast_fusion = (bf16[8,16,8,128]{3,2,1,0:T(8,128)(2,1)S(1)}, bf16[8,16,8,128]{3,2,1,0:T(8,128)(2,1)S(1)}, bf16[8,16,8,128]{3,2,1,0:T(8,128)(2,1)S(1)}, ...) fusion(bf16[64,16384]{1,0:T(8,128)(2,1)} %param.4), kind=kLoop, calls=%fused_computation.165 | loop fusion | bytes 4194304
  28.5 1.2 %fusion.48 = f32[64,128,128]{2,0,1:T(8,128)S(1)} fusion(f32[16,64,256]{2,1,0:T(8,128)S(1)} %get-tuple-element.19, f32[16,64]{1,0:T(8,128)S(1)} %broadcast_maximum_fusion.15, bf16[256,1024]{1,0:T(8,128)(2,1)} %all_gather.7), kind=kOutput, calls=%fused_computation.84 | convolution fusion | flops 67633152 | bytes 1642496 | tf_op jit(solution)/shard_map/grk,kd->rgd/dot_general | solution.py:40
  29.7 1.2 %fusion.154 = (f32[16,64]{1,0:T(8,128)S(1)}, f32[16,64,256]{2,1,0:T(8,128)S(1)}) fusion(bf16[8,16,8,128]{3,2,1,0:T(8,128)(2,1)S(1)} %get-tuple-element.8, bf16[256,1024]{1,0:T(8,128)(2,1)} %copy-done.10, pred[64,256]{1,0:T(8,128)(4,1)S(1)} %get-tuple-element.17), kind=kOutput, calls=%fused_computation.294 | convolution fusion | flops 67894272 | bytes 1396736 | tf_op jit(solution)/shard_map/rgd,kd->grk/dot_general | solution.py:32
  31.0 1.2 %fusion.152 = (f32[16,64]{1,0:T(8,128)S(1)}, f32[16,64,256]{2,1,0:T(8,128)S(1)}) fusion(bf16[8,16,8,128]{3,2,1,0:T(8,128)(2,1)S(1)} %get-tuple-element.9, bf16[256,1024]{1,0:T(8,128)(2,1)} %copy-done.10, pred[64,256]{1,0:T(8,128)(4,1)S(1)} %get-tuple-element.17), kind=kOutput, calls=%fused_computation.292 | convolution fusion | flops 67894272 | bytes 1396736 | tf_op jit(solution)/shard_map/rgd,kd->grk/dot_general | solution.py:32
  32.2 1.2 %fusion.151 = (f32[16,64]{1,0:T(8,128)S(1)}, f32[16,64,256]{2,1,0:T(8,128)S(1)}) fusion(bf16[8,16,8,128]{3,2,1,0:T(8,128)(2,1)S(1)} %get-tuple-element.10, bf16[256,1024]{1,0:T(8,128)(2,1)} %copy-done.10, pred[64,256]{1,0:T(8,128)(4,1)S(1)} %get-tuple-element.17), kind=kOutput, calls=%fused_computation.291 | convolution fusion | flops 67894272 | bytes 1396736 | tf_op jit(solution)/shard_map/rgd,kd->grk/dot_general | solution.py:32
  33.5 1.2 %fusion.150 = (f32[16,64]{1,0:T(8,128)S(1)}, f32[16,64,256]{2,1,0:T(8,128)S(1)}) fusion(bf16[8,16,8,128]{3,2,1,0:T(8,128)(2,1)S(1)} %get-tuple-element.11, bf16[256,1024]{1,0:T(8,128)(2,1)} %copy-done.10, pred[64,256]{1,0:T(8,128)(4,1)S(1)} %get-tuple-element.17), kind=kOutput, calls=%fused_computation.290 | convolution fusion | flops 67894272 | bytes 1396736 | tf_op jit(solution)/shard_map/rgd,kd->grk/dot_general | solution.py:32
  34.7 1.2 %fusion.149 = (f32[16,64]{1,0:T(8,128)S(1)}, f32[16,64,256]{2,1,0:T(8,128)S(1)}) fusion(bf16[8,16,8,128]{3,2,1,0:T(8,128)(2,1)S(1)} %get-tuple-element.12, bf16[256,1024]{1,0:T(8,128)(2,1)} %copy-done.10, pred[64,256]{1,0:T(8,128)(4,1)S(1)} %get-tuple-element.17), kind=kOutput, calls=%fused_computation.289 | convolution fusion | flops 67894272 | bytes 1396736 | tf_op jit(solution)/shard_map/rgd,kd->grk/dot_general | solution.py:32
  36.0 1.2 %fusion.148 = (f32[16,64]{1,0:T(8,128)S(1)}, f32[16,64,256]{2,1,0:T(8,128)S(1)}) fusion(bf16[8,16,8,128]{3,2,1,0:T(8,128)(2,1)S(1)} %get-tuple-element.13, bf16[256,1024]{1,0:T(8,128)(2,1)} %copy-done.10, pred[64,256]{1,0:T(8,128)(4,1)S(1)} %get-tuple-element.17), kind=kOutput, calls=%fused_computation.288 | convolution fusion | flops 67894272 | bytes 1396736 | tf_op jit(solution)/shard_map/rgd,kd->grk/dot_general | solution.py:32
  37.2 1.2 %fusion.153 = (f32[16,64]{1,0:T(8,128)S(1)}, f32[16,64,256]{2,1,0:T(8,128)S(1)}) fusion(bf16[8,16,8,128]{3,2,1,0:T(8,128)(2,1)S(1)} %get-tuple-element.15, bf16[256,1024]{1,0:T(8,128)(2,1)} %copy-done.10, pred[64,256]{1,0:T(8,128)(4,1)S(1)} %get-tuple-element.17), kind=kOutput, calls=%fused_computation.293 | convolution fusion | flops 67894272 | bytes 1396736 | tf_op jit(solution)/shard_map/rgd,kd->grk/dot_general | solution.py:32
  45.4 1.2 %fusion.43 = f32[64,128,128]{2,0,1:T(8,128)S(1)} fusion(f32[64,128,128]{2,0,1:T(8,128)S(1)} %fusion.44, f32[16,64,256]{2,1,0:T(8,128)S(1)} %get-tuple-element.29, f32[16,64]{1,0:T(8,128)S(1)} %broadcast_maximum_fusion.10, bf16[256,1024]{1,0:T(8,128)(2,1)} %all_gather.7), kind=kOutput, calls=%fused_computation.74 | convolution fusion | flops 67633152 | bytes 1646592 | tf_op jit(solution)/shard_map/grk,kd->rgd/dot_general | solution.py:40
  48.7 1.2 %fusion.41 = f32[64,128,128]{2,0,1:T(8,128)S(1)} fusion(f32[64,128,128]{2,0,1:T(8,128)S(1)} %fusion.42, f32[16,64,256]{2,1,0:T(8,128)S(1)} %get-tuple-element.33, f32[16,64]{1,0:T(8,128)S(1)} %broadcast_maximum_fusion.8, bf16[256,1024]{1,0:T(8,128)(2,1)} %all_gather.7), kind=kOutput, calls=%fused_computation.70 | convolution fusion | flops 67633152 | bytes 1646592 | tf_op jit(solution)/shard_map/grk,kd->rgd/dot_general | solution.py:40
  50.9 1.3 %fusion.160 = (f32[16,64]{1,0:T(8,128)S(1)}, f32[16,64,256]{2,1,0:T(8,128)S(1)}) fusion(bf16[8,16,8,128]{3,2,1,0:T(8,128)(2,1)S(1)} %get-tuple-element.9, bf16[256,1024]{1,0:T(8,128)(2,1)} %copy-done.11, pred[64,256]{1,0:T(8,128)(4,1)S(1)} %get-tuple-element.16), kind=kOutput, calls=%fused_computation.300 | convolution fusion | flops 67894272 | bytes 1396736 | tf_op jit(solution)/shard_map/rgd,kd->grk/dot_general | solution.py:32
  52.2 1.2 %fusion.159 = (f32[16,64]{1,0:T(8,128)S(1)}, f32[16,64,256]{2,1,0:T(8,128)S(1)}) fusion(bf16[8,16,8,128]{3,2,1,0:T(8,128)(2,1)S(1)} %get-tuple-element.10, bf16[256,1024]{1,0:T(8,128)(2,1)} %copy-done.11, pred[64,256]{1,0:T(8,128)(4,1)S(1)} %get-tuple-element.16), kind=kOutput, calls=%fused_computation.299 | convolution fusion | flops 67894272 | bytes 1396736 | tf_op jit(solution)/shard_map/rgd,kd->grk/dot_general | solution.py:32
  53.5 1.3 %fusion.158 = (f32[16,64]{1,0:T(8,128)S(1)}, f32[16,64,256]{2,1,0:T(8,128)S(1)}) fusion(bf16[8,16,8,128]{3,2,1,0:T(8,128)(2,1)S(1)} %get-tuple-element.11, bf16[256,1024]{1,0:T(8,128)(2,1)} %copy-done.11, pred[64,256]{1,0:T(8,128)(4,1)S(1)} %get-tuple-element.16), kind=kOutput, calls=%fused_computation.298 | convolution fusion | flops 67894272 | bytes 1396736 | tf_op jit(solution)/shard_map/rgd,kd->grk/dot_general | solution.py:32
  54.8 1.3 %fusion.157 = (f32[16,64]{1,0:T(8,128)S(1)}, f32[16,64,256]{2,1,0:T(8,128)S(1)}) fusion(bf16[8,16,8,128]{3,2,1,0:T(8,128)(2,1)S(1)} %get-tuple-element.12, bf16[256,1024]{1,0:T(8,128)(2,1)} %copy-done.11, pred[64,256]{1,0:T(8,128)(4,1)S(1)} %get-tuple-element.16), kind=kOutput, calls=%fused_computation.297 | convolution fusion | flops 67894272 | bytes 1396736 | tf_op jit(solution)/shard_map/rgd,kd->grk/dot_general | solution.py:32
  56.2 1.3 %fusion.156 = (f32[16,64]{1,0:T(8,128)S(1)}, f32[16,64,256]{2,1,0:T(8,128)S(1)}) fusion(bf16[8,16,8,128]{3,2,1,0:T(8,128)(2,1)S(1)} %get-tuple-element.13, bf16[256,1024]{1,0:T(8,128)(2,1)} %copy-done.11, pred[64,256]{1,0:T(8,128)(4,1)S(1)} %get-tuple-element.16), kind=kOutput, calls=%fused_computation.296 | convolution fusion | flops 67894272 | bytes 1396736 | tf_op jit(solution)/shard_map/rgd,kd->grk/dot_general | solution.py:32
  58.0 1.2 %fusion.161 = (f32[16,64]{1,0:T(8,128)S(1)}, f32[16,64,256]{2,1,0:T(8,128)S(1)}) fusion(bf16[8,16,8,128]{3,2,1,0:T(8,128)(2,1)S(1)} %get-tuple-element.15, bf16[256,1024]{1,0:T(8,128)(2,1)} %copy-done.11, pred[64,256]{1,0:T(8,128)(4,1)S(1)} %get-tuple-element.16), kind=kOutput, calls=%fused_computation.301 | convolution fusion | flops 67894272 | bytes 1396736 | tf_op jit(solution)/shard_map/rgd,kd->grk/dot_general | solution.py:32
  63.2 1.3 %fusion.40 = f32[64,128,128]{2,0,1:T(8,128)S(1)} fusion(f32[16,64,256]{2,1,0:T(8,128)S(1)} %get-tuple-element.35, f32[16,64]{1,0:T(8,128)S(1)} %broadcast_maximum_fusion.7, bf16[256,1024]{1,0:T(8,128)(2,1)} %collective-permute-done.1), kind=kOutput, calls=%fused_computation.68 | convolution fusion | flops 67633152 | bytes 1642496 | tf_op jit(solution)/shard_map/grk,kd->rgd/dot_general | solution.py:40
  64.5 1.7 %fusion.39 = f32[64,128,128]{2,0,1:T(8,128)S(1)} fusion(f32[64,128,128]{2,0,1:T(8,128)S(1)} %fusion.40, f32[16,64,256]{2,1,0:T(8,128)} %copy-done.5, f32[16,64]{1,0:T(8,128)S(1)} %broadcast_maximum_fusion.6, bf16[256,1024]{1,0:T(8,128)(2,1)} %collective-permute-done.1), kind=kOutput, calls=%fused_computation.66 | convolution fusion | flops 67633152 | bytes 1646592 | tf_op jit(solution)/shard_map/grk,kd->rgd/dot_general | solution.py:40
  66.2 1.6 %fusion.38 = f32[64,128,128]{2,0,1:T(8,128)S(1)} fusion(f32[64,128,128]{2,0,1:T(8,128)S(1)} %fusion.39, f32[16,64,256]{2,1,0:T(8,128)} %copy-done.4, f32[16,64]{1,0:T(8,128)S(1)} %broadcast_maximum_fusion.5, bf16[256,1024]{1,0:T(8,128)(2,1)} %collective-permute-done.1), kind=kOutput, calls=%fused_computation.64 | convolution fusion | flops 67633152 | bytes 1646592 | tf_op jit(solution)/shard_map/grk,kd->rgd/dot_general | solution.py:40
  67.8 1.3 %fusion.37 = f32[64,128,128]{2,0,1:T(8,128)S(1)} fusion(f32[64,128,128]{2,0,1:T(8,128)S(1)} %fusion.38, f32[16,64,256]{2,1,0:T(8,128)S(1)} %copy-done.3, f32[16,64]{1,0:T(8,128)S(1)} %broadcast_maximum_fusion.4, bf16[256,1024]{1,0:T(8,128)(2,1)} %collective-permute-done.1), kind=kOutput, calls=%fused_computation.62 | convolution fusion | flops 67633152 | bytes 1646592 | tf_op jit(solution)/shard_map/grk,kd->rgd/dot_general | solution.py:40
  69.2 1.2 %fusion.36 = f32[64,128,128]{2,0,1:T(8,128)S(1)} fusion(f32[64,128,128]{2,0,1:T(8,128)S(1)} %fusion.37, f32[16,64,256]{2,1,0:T(8,128)S(1)} %copy-done.1, f32[16,64]{1,0:T(8,128)S(1)} %broadcast_maximum_fusion.3, bf16[256,1024]{1,0:T(8,128)(2,1)} %collective-permute-done.1), kind=kOutput, calls=%fused_computation.60 | convolution fusion | flops 67633152 | bytes 1646592 | tf_op jit(solution)/shard_map/grk,kd->rgd/dot_general | solution.py:40
  70.4 1.2 %fusion.35 = f32[64,128,128]{2,0,1:T(8,128)S(1)} fusion(f32[64,128,128]{2,0,1:T(8,128)S(1)} %fusion.36, f32[16,64,256]{2,1,0:T(8,128)S(1)} %get-tuple-element.45, f32[16,64]{1,0:T(8,128)S(1)} %broadcast_maximum_fusion.2, bf16[256,1024]{1,0:T(8,128)(2,1)} %collective-permute-done.1), kind=kOutput, calls=%fused_computation.58 | convolution fusion | flops 67633152 | bytes 1646592 | tf_op jit(solution)/shard_map/grk,kd->rgd/dot_general | solution.py:40
  71.6 1.2 %fusion.34 = f32[64,128,128]{2,0,1:T(8,128)S(1)} fusion(f32[64,128,128]{2,0,1:T(8,128)S(1)} %fusion.35, f32[16,64,256]{2,1,0:T(8,128)S(1)} %copy-done.7, f32[16,64]{1,0:T(8,128)S(1)} %broadcast_maximum_fusion.1, bf16[256,1024]{1,0:T(8,128)(2,1)} %collective-permute-done.1), kind=kOutput, calls=%fused_computation.56 | convolution fusion | flops 67633152 | bytes 1646592 | tf_op jit(solution)/shard_map/grk,kd->rgd/dot_general | solution.py:40
  74.0 5.2 %copy_bitcast_fusion = bf16[64,16384]{1,0:T(8,128)(2,1)} fusion(f32[64,128]{0,1:T(8,128)S(1)} %get-tuple-element.5, f32[64,128,128]{2,0,1:T(8,128)S(1)} %fusion.33, f32[64,128]{0,1:T(8,128)S(1)} %get-tuple-element.7, f32[64,128,128]{2,0,1:T(8,128)S(1)} %copy-done.9, f32[64,128]{0,1:T(8,128)S(1)} %get-tuple-element.6), kind=kLoop, calls=%fused_computation.3 | loop fusion | flops 5242880 | bytes 10584064 | tf_op jit(solution)/shard_map/convert_element_type | solution.py:92
  (112 shorter events, 16.5 us)
Async XLA Ops:
  10.8 52.3 %collective-permute-start.1 = (bf16[256,1024]{1,0:T(8,128)(2,1)}, bf16[256,1024]{1,0:T(8,128)(2,1)}, u32[]{:S(2)}, u32[]{:S(2)}) collective-permute-start(bf16[256,1024]{1,0:T(8,128)(2,1)} %all_gather.7), channel_id=1, source_target_pairs={{7,0},{0,1},{1,2},{2,3},{3,4},{4,5},{5,6},{6,7},{15,8},{8,9},{9,10... | collective-permute-start | bytes 1572872 | tf_op jit(solution)/shard_map/ppermute | solution.py:14
  19.6 10.2 %copy-start.10 = (bf16[256,1024]{1,0:T(8,128)(2,1)}, bf16[256,1024]{1,0:T(8,128)(2,1)S(1)}, u32[]{:S(2)}) copy-start(bf16[256,1024]{1,0:T(8,128)(2,1)S(1)} %all_gather.6) | copy-start | bytes 1572868
  19.6 30.3 %collective-permute-start = (bf16[256,1024]{1,0:T(8,128)(2,1)S(1)}, bf16[256,1024]{1,0:T(8,128)(2,1)S(1)}, u32[]{:S(2)}, u32[]{:S(2)}) collective-permute-start(bf16[256,1024]{1,0:T(8,128)(2,1)S(1)} %all_gather.6), channel_id=1, source_target_pairs={{7,0},{0,1},{1,2},{2,3},{3,4},{4,5},{5,6},{6,7},{15,8},{8,9},{9,10... | collective-permute-start | bytes 1572872 | tf_op jit(solution)/shard_map/ppermute | solution.py:14
  49.9 6.3 %copy-start.8 = (f32[64,128,128]{2,0,1:T(8,128)}, f32[64,128,128]{2,0,1:T(8,128)S(1)}, u32[]{:S(2)}) copy-start(f32[64,128,128]{2,0,1:T(8,128)S(1)} %fusion.41) | copy-start | bytes 12582916
  49.9 1.0 %copy-start.11 = (bf16[256,1024]{1,0:T(8,128)(2,1)}, bf16[256,1024]{1,0:T(8,128)(2,1)S(1)}, u32[]{:S(2)}) copy-start(bf16[256,1024]{1,0:T(8,128)(2,1)S(1)} %collective-permute-done) | copy-start | bytes 1572868
  53.4 6.6 %copy-start = (f32[16,64,256]{2,1,0:T(8,128)}, f32[16,64,256]{2,1,0:T(8,128)S(1)}, u32[]{:S(2)}) copy-start(f32[16,64,256]{2,1,0:T(8,128)S(1)} %get-tuple-element.43) | copy-start | bytes 3145732
  54.8 5.7 %copy-start.2 = (f32[16,64,256]{2,1,0:T(8,128)}, f32[16,64,256]{2,1,0:T(8,128)S(1)}, u32[]{:S(2)}) copy-start(f32[16,64,256]{2,1,0:T(8,128)S(1)} %get-tuple-element.41) | copy-start | bytes 3145732
  56.1 5.3 %copy-start.4 = (f32[16,64,256]{2,1,0:T(8,128)}, f32[16,64,256]{2,1,0:T(8,128)S(1)}, u32[]{:S(2)}) copy-start(f32[16,64,256]{2,1,0:T(8,128)S(1)} %get-tuple-element.39) | copy-start | bytes 3145732
  57.5 4.5 %copy-start.5 = (f32[16,64,256]{2,1,0:T(8,128)}, f32[16,64,256]{2,1,0:T(8,128)S(1)}, u32[]{:S(2)}) copy-start(f32[16,64,256]{2,1,0:T(8,128)S(1)} %get-tuple-element.37) | copy-start | bytes 3145732
  59.2 2.8 %copy-start.6 = (f32[16,64,256]{2,1,0:T(8,128)}, f32[16,64,256]{2,1,0:T(8,128)S(1)}, u32[]{:S(2)}) copy-start(f32[16,64,256]{2,1,0:T(8,128)S(1)} %get-tuple-element.47) | copy-start | bytes 3145732
  63.1 4.6 %copy-start.3 = (f32[16,64,256]{2,1,0:T(8,128)S(1)}, f32[16,64,256]{2,1,0:T(8,128)}, u32[]{:S(2)}) copy-start(f32[16,64,256]{2,1,0:T(8,128)} %copy-done.2) | copy-start | bytes 3145732
  63.1 6.0 %copy-start.1 = (f32[16,64,256]{2,1,0:T(8,128)S(1)}, f32[16,64,256]{2,1,0:T(8,128)}, u32[]{:S(2)}) copy-start(f32[16,64,256]{2,1,0:T(8,128)} %copy-done) | copy-start | bytes 3145732
  64.5 7.1 %copy-start.7 = (f32[16,64,256]{2,1,0:T(8,128)S(1)}, f32[16,64,256]{2,1,0:T(8,128)}, u32[]{:S(2)}) copy-start(f32[16,64,256]{2,1,0:T(8,128)} %copy-done.6) | copy-start | bytes 3145732
  67.8 6.2 %copy-start.9 = (f32[64,128,128]{2,0,1:T(8,128)S(1)}, f32[64,128,128]{2,0,1:T(8,128)}, u32[]{:S(2)}) copy-start(f32[64,128,128]{2,0,1:T(8,128)} %copy-done.8) | copy-start | bytes 12582916
where the time goes:
time: 80.7 us; the launch traced here: 79.2 us
  matrix products  37.8 us (47%)
  blocking collectives  17.4 us (22%)
  other arithmetic  12.2 us (15%)
  local copies, waits for them, and re-layouts  6.59 us (8%)
  starting transfers between devices  3.04 us (4%)
  between operations  2.19 us (3%)
    dot_general x16, matrix products, partial_terms(): jnp.einsum('grk,kd->rgd', probs, v_head, preferred_element_type=jnp.float32)  20.3 us
    dot_general x16, matrix products, partial_terms(): jnp.einsum('rgd,kd->grk', q_head, key_head_index, preferred_element_type=...  17.5 us
    all_gather x1, blocking collectives, body(): lax.all_gather(value, 'head', axis=0, tiled=True)  10.2 us
    all_gather x1, blocking collectives, body(): lax.all_gather(key, 'head', axis=0, tiled=True)  7.2 us
    reduce_sum x16, other arithmetic, partial_terms(): total = jnp.sum(weights, axis=-1)  6.54 us
    convert_element_type x1, other arithmetic, body(): return (result.astype(jnp.bfloat16), lse)  5.21 us
    ppermute x2, starting transfers between devices, passed_along(): return lax.ppermute(block, axis, route)  3.04 us
    unnamed x40, local copies, waits for them, and re-layouts  2.59 us
  transfers between devices with their start and end apart: 2, of which 0 were waited for; matrix products, arithmetic and copies ran while one was open for 51% of the time, Pallas kernels for 0%

commit v1 on v0

v1 whole, which is shorter than its diff:
```python
import functools
import math

import jax
import jax.numpy as jnp
from jax import lax
from jax.experimental import pallas as pl
from jax.experimental.pallas import tpu as pltpu
from jax.sharding import PartitionSpec as P

HEAD_DIMENSION = 128
MASKED = -1e30
FLOOR = -10000.0
GROUPS_PER_DOT = 4
MESH = pl.DeviceIdType.MESH


def kernel(
    n_head,
    n_ctx,
    order_ref,
    q_hbm,
    k_hbm,
    v_hbm,
    out_ref,
    lse_ref,
    qbuf,
    kbuf,
    vbuf,
    bias_ref,
    m_ref,
    l_ref,
    q_sem,
    own_sem,
    send_sem,
    recv_sem,
):
    d = HEAD_DIMENSION
    block = k_hbm.shape[0]
    kv_heads = k_hbm.shape[1] // d
    width = q_hbm.shape[1] // kv_heads
    group = width // d
    chips = n_head // 2
    slots = 2 * n_head
    n_keys = slots * block
    head = lax.axis_index("head")
    ctx = lax.axis_index("ctx")
    chip, core = lax.div(head, 2), lax.rem(head, 2)
    sibling_head = chip * 2 + (1 - core)
    next_ctx = lax.rem(ctx + 1, n_ctx)
    prev_ctx = lax.rem(ctx + n_ctx - 1, n_ctx)

    def chip_head(j):
        return lax.rem(chip + j, chips) * 2 + core

    def slot_of(p, j, s):
        return (p * chips + j) * 2 + s

    bufs = (kbuf, vbuf)

    def local_q(h):
        cols = pl.ds(pl.multiple_of(h * width, width), width)
        return pltpu.make_async_copy(q_hbm.at[:, cols], qbuf.at[h], q_sem.at[h])

    def local_kv(h, kv):
        cols = pl.ds(pl.multiple_of(h * d, d), d)
        src = (k_hbm, v_hbm)[kv]
        return pltpu.make_async_copy(src.at[:, cols], bufs[kv].at[h, 0], own_sem.at[h, kv])

    def remote(h, kv, src_slot, dst_slot, to_head, to_ctx):
        return pltpu.make_async_remote_copy(
            src_ref=bufs[kv].at[h, src_slot],
            dst_ref=bufs[kv].at[h, dst_slot],
            send_sem=send_sem.at[dst_slot, h, kv],
            recv_sem=recv_sem.at[dst_slot, h, kv],
            device_id=(to_head, to_ctx),
            device_id_type=MESH,
        )

    def to_sibling(h, kv, slot):
        return remote(h, kv, slot, slot + 1, sibling_head, ctx)

    def own_across(h, kv, j):
        return remote(h, kv, 0, slot_of(0, j, 0), chip_head(j), ctx)

    def own_onward(h, kv):
        return remote(h, kv, 0, slot_of(1, 0, 0), head, next_ctx)

    def relayed(h, kv, j):
        if kv == 0:
            return remote(h, 0, slot_of(1, 0, 0), slot_of(1, j, 0), chip_head(j), ctx)
        return remote(h, 1, slot_of(0, j, 0), slot_of(1, j, 0), head, next_ctx)

    def all_copies(h, kv):
        made = [own_onward(h, kv), to_sibling(h, kv, 0)]
        made += [own_across(h, kv, j) for j in range(1, chips)]
        made += [to_sibling(h, kv, slot_of(1, 0, 0))]
        for j in range(1, chips):
            made += [relayed(h, kv, j), to_sibling(h, kv, slot_of(0, j, 0)), to_sibling(h, kv, slot_of(1, j, 0))]
        return made

    for h in range(kv_heads):
        for kv in range(2):
            local_kv(h, kv).start()
    for h in range(kv_heads):
        local_q(h).start()

    barrier = pltpu.get_barrier_semaphore()
    pl.semaphore_signal(barrier, inc=1, device_id=(sibling_head, ctx), device_id_type=MESH)
    for j in range(1, chips):
        pl.semaphore_signal(barrier, inc=1, device_id=(chip_head(j), ctx), device_id_type=MESH)
    pl.semaphore_signal(barrier, inc=1, device_id=(head, next_ctx), device_id_type=MESH)
    pl.semaphore_signal(barrier, inc=1, device_id=(head, prev_ctx), device_id_type=MESH)

    rows = lax.broadcasted_iota(jnp.int32, (block, n_keys), 0)
    cols = lax.broadcasted_iota(jnp.int32, (block, n_keys), 1)
    key_slot, key_row = cols // block, cols % block
    key_block = jnp.zeros((block, n_keys), jnp.int32)
    for p in range(2):
        from_ctx = ctx if p == 0 else prev_ctx
        for j in range(chips):
            from_chip = lax.rem(chip + chips - j, chips)
            for s in range(2):
                from_head = from_chip * 2 + (core if s == 0 else 1 - core)
                stored = order_ref[from_head * n_ctx + from_ctx]
                key_block = jnp.where(key_slot == slot_of(p, j, s), stored, key_block)
    my_block = order_ref[head * n_ctx + ctx]
    visible = key_block * block + key_row <= my_block * block + rows
    bias_ref[...] = jnp.where(visible, 0.0, MASKED).astype(jnp.float32)
    m_ref[...] = jnp.zeros_like(m_ref)
    l_ref[...] = jnp.ones_like(l_ref)

    pl.semaphore_wait(barrier, chips + 2)

    def send_own(h):
        for kv in range(2):
            local_kv(h, kv).wait()
        for kv in range(2):
            for j in range(1, chips):
                own_across(h, kv, j).start()
            own_onward(h, kv).start()
            to_sibling(h, kv, 0).start()

    def first_hop(h):
        for kv in range(2):
            own_onward(h, kv).wait_recv()
            for j in range(1, chips):
                own_across(h, kv, j).wait_recv()
            for j in range(1, chips):
                relayed(h, kv, j).start()
            to_sibling(h, kv, slot_of(1, 0, 0)).start()
            for j in range(1, chips):
                to_sibling(h, kv, slot_of(0, j, 0)).start()

    def second_hop(h):
        for kv in range(2):
            for j in range(1, chips):
                relayed(h, kv, j).wait_recv()
                to_sibling(h, kv, slot_of(1, j, 0)).start()

    def last_hop(h):
        for kv in range(2):
            for p in range(2):
                for j in range(chips):
                    to_sibling(h, kv, slot_of(p, j, 0)).wait_recv()

    scale = 1.0 / math.sqrt(d)
    exp_scale = scale * math.log2(math.e)
    lane = lax.broadcasted_iota(jnp.int32, (block, lse_ref.shape[1]), 1)

    def attend(h):
        local_q(h).wait()
        k_h = kbuf[h].reshape(n_keys, d)
        v_h = vbuf[h].reshape(n_keys, d)
        v_ones = jnp.concatenate([v_h, jnp.ones_like(v_h)], axis=1)
        bias = bias_ref[...]
        m_all, l_all = m_ref[...], l_ref[...]
        for first in range(0, group, GROUPS_PER_DOT):
            members = range(first, min(first + GROUPS_PER_DOT, group))
            q = jnp.concatenate([qbuf[h, :, g * d : (g + 1) * d] for g in members], axis=0)
            s = lax.dot_general(q, k_h, (((1,), (1,)), ((), ())), preferred_element_type=jnp.float32)
            s = s.reshape(len(members), block, n_keys) + bias[None]
            m = jnp.maximum(jnp.max(s, axis=-1, keepdims=True), FLOOR / scale)
            probs = jnp.exp2((s - m) * exp_scale).astype(jnp.bfloat16)
            o = jnp.dot(
                probs.reshape(len(members) * block, n_keys), v_ones, preferred_element_type=jnp.float32
            )
            for i, g in enumerate(members):
                acc = o[i * block : (i + 1) * block, :d]
                total = o[i * block : (i + 1) * block, d:]
                start = pl.multiple_of(h * width + g * d, d)
                out_ref[:, pl.ds(start, d)] = (acc / total).astype(out_ref.dtype)
                here = lane == h * group + g
                m_all = jnp.where(here, m[i], m_all)
                l_all = jnp.where(here, total[:, :1], l_all)
        m_ref[...] = m_all
        l_ref[...] = l_all

    ahead = 3
    for h in range(min(ahead, kv_heads)):
        send_own(h)

    def stage(i, carry):
        t = i - 2

        @pl.when(t + 2 < kv_heads)
        def _():
            first_hop(t + 2)

        @pl.when(t + 2 + 1 < kv_heads)
        def _():
            @pl.when(t + 2 + 1 >= ahead)
            def _():
                send_own(t + 2 + 1)

        @pl.when(jnp.logical_and(t + 1 >= 0, t + 1 < kv_heads))
        def _():
            second_hop(t + 1)

        @pl.when(t >= 0)
        def _():
            last_hop(t)
            attend(t)

        return carry

    lax.fori_loop(0, kv_heads + 2, stage, 0)
    lse_ref[...] = m_ref[...] * scale + jnp.log(l_ref[...])

    def drain(h, carry):
        for kv in range(2):
            for copy in all_copies(h, kv):
                copy.wait_send()
        return carry

    lax.fori_loop(0, kv_heads, drain, 0)


def body(query, key, value, block_order):
    n_head = lax.axis_size("head")
    n_ctx = lax.axis_size("ctx")
    block, q_width = query.shape
    d = HEAD_DIMENSION
    kv_heads = key.shape[1] // d
    q_heads = q_width // d
    slots = 2 * n_head
    anywhere = pl.BlockSpec(memory_space=pl.ANY)
    vmem = pl.BlockSpec(memory_space=pltpu.VMEM)
    return pl.pallas_call(
        functools.partial(kernel, n_head, n_ctx),
        out_shape=(
            jax.ShapeDtypeStruct((block, q_width), jnp.bfloat16),
            jax.ShapeDtypeStruct((block, q_heads), jnp.float32),
        ),
        in_specs=[pl.BlockSpec(memory_space=pltpu.SMEM), anywhere, anywhere, anywhere],
        out_specs=(vmem, vmem),
        scratch_shapes=[
            pltpu.VMEM((kv_heads, block, q_width // kv_heads), jnp.bfloat16),
            pltpu.VMEM((kv_heads, slots, block, d), jnp.bfloat16),
            pltpu.VMEM((kv_heads, slots, block, d), jnp.bfloat16),
            pltpu.VMEM((block, slots * block), jnp.float32),
            pltpu.VMEM((block, q_heads), jnp.float32),
            pltpu.VMEM((block, q_heads), jnp.float32),
            pltpu.SemaphoreType.DMA((kv_heads,)),
            pltpu.SemaphoreType.DMA((kv_heads, 2)),
            pltpu.SemaphoreType.DMA((slots, kv_heads, 2)),
            pltpu.SemaphoreType.DMA((slots, kv_heads, 2)),
        ],
        compiler_params=pltpu.CompilerParams(collective_id=0, has_side_effects=True),
    )(block_order, query, key, value)


def solution(mesh):
    placed = (P(("head", "ctx"), None), P(("head", "ctx"), None), P(("head", "ctx"), None), P())
    return jax.shard_map(
        body,
        mesh=mesh,
        in_specs=placed,
        out_specs=(P(("head", "ctx"), None), P(("head", "ctx"), None)),
        check_vma=False,
    )
```

time: 80.7 us -> 44.4 us (0.55); the launches traced: 79.2 us -> 44.3 us
  Pallas kernels: 0 us -> 40 us
  matrix products: 37.8 us -> 0 us
  blocking collectives: 17.4 us -> 0 us
  other arithmetic: 12.2 us -> 0 us
  starting transfers between devices: 3.04 us -> 0 us
  local copies, waits for them, and re-layouts: 6.59 us -> 3.67 us
  between operations: 2.19 us -> 0.65 us
    pallas_call x0 -> x1, Pallas kernels: none -> 40 us  [body(): pl.pallas_call(functools.partial(kernel, n_head, n_ctx), out_shape=(jax.S...]
    dot_general x32 -> x0, matrix products: 37.8 us -> none  [the longest x16 20.3 us: partial_terms(): jnp.einsum('grk,kd->rgd', probs, v_head, preferred_element_type=jnp.float32)]
    all_gather x2 -> x0, blocking collectives: 17.4 us -> none  [the longest x1 10.2 us: body(): lax.all_gather(value, 'head', axis=0, tiled=True)]
    reduce_sum x16 -> x0, other arithmetic: 6.54 us -> none  [partial_terms(): total = jnp.sum(weights, axis=-1)]
    convert_element_type x1 -> x0, other arithmetic: 5.21 us -> none  [body(): return (result.astype(jnp.bfloat16), lse)]
    ppermute x2 -> x0, starting transfers between devices: 3.04 us -> none  [passed_along(): return lax.ppermute(block, axis, route)]
    gather x2 -> x0, local copies, waits for them, and re-layouts: 2.59 us -> none  [shard_positions(): starts = block_order[stored] * block]
    dynamic_slice x1 -> x0, local copies, waits for them, and re-layouts: 1.24 us -> none  [body(): block_order[here_head * n_ctx + here_ctx] * block + offsets]
  transfers between devices with their start and end apart: 2 -> 0, of which waited for: 0 -> 0; matrix products, arithmetic and copies ran while one was open for 51% -> 0% of each run, Pallas kernels for 0% -> 0%
where the time goes in v1:
time: 44.4 us; the launch traced here: 44.3 us
  Pallas kernels  40 us (90%)
  local copies, waits for them, and re-layouts  3.67 us (8%)
  between operations  0.65 us (1%)
    pallas_call x1, Pallas kernels, body(): pl.pallas_call(functools.partial(kernel, n_head, n_ctx), out_shape=(jax.S...  40 us
    unnamed x4, local copies, waits for them, and re-layouts  3.67 us

profile of v1, /device:TPU:0, one launch (start us, length us, event | category | flops | bytes accessed | tf_op | source)
XLA Modules:
  0.0 44.3 jit_solution(2549229273697319494)
XLA Ops:
  0.6 40.0 %shard_map.59 = (bf16[64,16384]{1,0:T(8,128)(2,1)}, f32[64,128]{1,0:T(8,128)}) custom-call(s32[32]{0:T(128)} %order_ref.1, bf16[64,16384]{1,0:T(8,128)(2,1)} %q_hbm.1, bf16[64,1024]{1,0:T(8,128)(2,1)} %k_hbm.1, bf16[64,1024]{1,0:T(8,128)(2,1)} %v_hbm.1), custom_call_target="tpu_custom_call" | custom-call | tf_op jit(solution)/shard_map/pallas_call | solution.py:249
  40.6 0.0 copy-start
  40.6 3.0 %copy.8 = bf16[64,16384]{1,0:T(8,128)(2,1)} copy(bf16[64,16384]{1,0:T(8,128)(2,1)} %get-tuple-element.4) | data formatting | bytes 4194304
  43.7 0.0 copy-done
  43.7 0.6 %copy.9 = f32[64,128]{1,0:T(8,128)} copy(f32[64,128]{1,0:T(8,128)S(1)} %copy-done) | data formatting | bytes 65536
Async XLA Ops:
  40.6 3.1 %copy-start = (f32[64,128]{1,0:T(8,128)S(1)}, f32[64,128]{1,0:T(8,128)}, u32[]{:S(2)}) copy-start(f32[64,128]{1,0:T(8,128)} %get-tuple-element.5) | copy-start | bytes 98308

commit v2 on v0

v2 whole, which is shorter than its diff:
```python
import functools
import math

import jax
import jax.numpy as jnp
from jax import lax
from jax.experimental import pallas as pl
from jax.experimental.pallas import tpu as pltpu
from jax.sharding import PartitionSpec as P

HEAD_DIMENSION = 128
MASKED = -1e30
FLOOR = -10000.0
GROUPS_PER_DOT = 4
HEADS_PER_PIECE = 4
AHEAD = 2
VMEM_LIMIT = 24 * 1024 * 1024
MESH = pl.DeviceIdType.MESH


def key_bias(order_ref, block, n_head, n_ctx):
    head = lax.axis_index("head")
    ctx = lax.axis_index("ctx")
    chips = n_head // 2
    chip, core = lax.div(head, 2), lax.rem(head, 2)
    prev_ctx = lax.rem(ctx + n_ctx - 1, n_ctx)
    n_keys = 2 * n_head * block
    rows = lax.broadcasted_iota(jnp.int32, (block, n_keys), 0)
    cols = lax.broadcasted_iota(jnp.int32, (block, n_keys), 1)
    key_slot, key_row = cols // block, cols % block
    key_block = jnp.zeros((block, n_keys), jnp.int32)
    for p in range(2):
        from_ctx = ctx if p == 0 else prev_ctx
        for j in range(chips):
            from_chip = lax.rem(chip + chips - j, chips)
            for s in range(2):
                from_head = from_chip * 2 + (core if s == 0 else 1 - core)
                stored = order_ref[from_head * n_ctx + from_ctx]
                key_block = jnp.where(key_slot == (p * chips + j) * 2 + s, stored, key_block)
    my_block = order_ref[head * n_ctx + ctx]
    visible = key_block * block + key_row <= my_block * block + rows
    return jnp.where(visible, 0.0, MASKED).astype(jnp.float32)


def attend_head(h, group, q_ref, k_h, v_h, bias_ref, m_ref, l_ref, lane, put):
    d = HEAD_DIMENSION
    scale = 1.0 / math.sqrt(d)
    exp_scale = scale * math.log2(math.e)
    block, n_keys = bias_ref.shape
    v_ones = jnp.concatenate([v_h, jnp.ones_like(v_h)], axis=1)
    bias = bias_ref[...]
    m_all, l_all = m_ref[...], l_ref[...]
    for first in range(0, group, GROUPS_PER_DOT):
        members = range(first, min(first + GROUPS_PER_DOT, group))
        q = jnp.concatenate([q_ref[:, g * d : (g + 1) * d] for g in members], axis=0)
        s = lax.dot_general(q, k_h, (((1,), (1,)), ((), ())), preferred_element_type=jnp.float32)
        s = s.reshape(len(members), block, n_keys) + bias[None]
        m = jnp.maximum(jnp.max(s, axis=-1, keepdims=True), FLOOR / scale)
        probs = jnp.exp2((s - m) * exp_scale).astype(jnp.bfloat16)
        o = jnp.dot(
            probs.reshape(len(members) * block, n_keys), v_ones, preferred_element_type=jnp.float32
        )
        for i, g in enumerate(members):
            acc = o[i * block : (i + 1) * block, :d]
            total = o[i * block : (i + 1) * block, d:]
            put(g, (acc / total).astype(jnp.bfloat16))
            here = lane == h * group + g
            m_all = jnp.where(here, m[i], m_all)
            l_all = jnp.where(here, total[:, :1], l_all)
    m_ref[...] = m_all
    l_ref[...] = l_all


def finish_kernel(
    early,
    bias_ref,
    q_hbm,
    kv_ref,
    early_ref,
    stats_ref,
    out_hbm,
    lse_ref,
    qbuf,
    obuf,
    m_ref,
    l_ref,
    q_sem,
    out_sem,
):
    d = HEAD_DIMENSION
    late, _, _, block, piece = kv_ref.shape
    per_piece = piece // d
    n_late = late * per_piece
    n_early = early * per_piece
    width = q_hbm.shape[1] // (n_late + n_early)
    group = width // d
    n_keys = bias_ref.shape[1]

    def fetch(h):
        return pltpu.make_async_copy(
            q_hbm.at[:, pl.ds((n_early + h) * width, width)], qbuf.at[h], q_sem.at[h]
        )

    def store(h):
        return pltpu.make_async_copy(
            obuf.at[h], out_hbm.at[:, pl.ds((n_early + h) * width, width)], out_sem.at[h]
        )

    for h in range(n_late):
        fetch(h).start()
    ready = pltpu.make_async_copy(early_ref, out_hbm.at[:, pl.ds(0, n_early * width)], out_sem.at[n_late])
    ready.start()
    m_ref[...] = stats_ref[0]
    l_ref[...] = stats_ref[1]
    lane = lax.broadcasted_iota(jnp.int32, m_ref.shape, 1)
    for h in range(n_late):
        c, sub = h // per_piece, h % per_piece
        fetch(h).wait()
        k_h = kv_ref[c, :, 0, :, sub * d : (sub + 1) * d].reshape(n_keys, d)
        v_h = kv_ref[c, :, 1, :, sub * d : (sub + 1) * d].reshape(n_keys, d)

        def put(g, tile, h=h):
            obuf[h, :, g * d : (g + 1) * d] = tile

        attend_head(n_early + h, group, qbuf.at[h], k_h, v_h, bias_ref, m_ref, l_ref, lane, put)
        store(h).start()
    lse_ref[...] = m_ref[...] * (1.0 / math.sqrt(d)) + jnp.log(l_ref[...])
    for h in range(n_late):
        store(h).wait()
    ready.wait()


def kernel(
    n_head,
    n_ctx,
    order_ref,
    q_hbm,
    k_hbm,
    v_hbm,
    out_ref,
    late_ref,
    stats_ref,
    bias_ref,
    qbuf,
    kvearly,
    q_sem,
    own_sem,
    send_sem,
    recv_sem,
):
    d = HEAD_DIMENSION
    block = k_hbm.shape[0]
    early, piece = kvearly.shape[0], kvearly.shape[4]
    pieces = early + late_ref.shape[0]
    m_ref, l_ref = stats_ref.at[0], stats_ref.at[1]
    per_piece = piece // d
    kv_heads = pieces * per_piece
    width = q_hbm.shape[1] // kv_heads
    group = width // d
    chips = n_head // 2
    slots = 2 * n_head
    n_keys = slots * block
    head = lax.axis_index("head")
    ctx = lax.axis_index("ctx")
    chip, core = lax.div(head, 2), lax.rem(head, 2)
    sibling_head = chip * 2 + (1 - core)
    next_ctx = lax.rem(ctx + 1, n_ctx)
    prev_ctx = lax.rem(ctx + n_ctx - 1, n_ctx)

    def chip_head(j):
        return lax.rem(chip + j, chips) * 2 + core

    def slot_of(p, j, s):
        return (p * chips + j) * 2 + s

    def piece_of(c):
        return kvearly.at[c] if c < early else late_ref.at[c - early]

    def local_q(h):
        cols = pl.ds(pl.multiple_of(h * width, width), width)
        return pltpu.make_async_copy(q_hbm.at[:, cols], qbuf.at[h], q_sem.at[h])

    def local_kv(c, kv):
        cols = pl.ds(pl.multiple_of(c * piece, piece), piece)
        src = (k_hbm, v_hbm)[kv]
        return pltpu.make_async_copy(src.at[:, cols], piece_of(c).at[0, kv], own_sem.at[c, kv])

    def remote(c, src_slot, dst_slot, to_head, to_ctx):
        return pltpu.make_async_remote_copy(
            src_ref=piece_of(c).at[src_slot],
            dst_ref=piece_of(c).at[dst_slot],
            send_sem=send_sem.at[dst_slot, c, 0],
            recv_sem=recv_sem.at[dst_slot, c, 0],
            device_id=(to_head, to_ctx),
            device_id_type=MESH,
        )

    def to_sibling(c, slot):
        return remote(c, slot, slot + 1, sibling_head, ctx)

    def own_across(c, j):
        return remote(c, 0, slot_of(0, j, 0), chip_head(j), ctx)

    def own_onward(c):
        return remote(c, 0, slot_of(1, 0, 0), head, next_ctx)

    def relayed(c, kv, j):
        src_slot = (slot_of(1, 0, 0), slot_of(0, j, 0))[kv]
        dst_slot = slot_of(1, j, 0)
        return pltpu.make_async_remote_copy(
            src_ref=piece_of(c).at[src_slot, kv],
            dst_ref=piece_of(c).at[dst_slot, kv],
            send_sem=send_sem.at[dst_slot, c, kv],
            recv_sem=recv_sem.at[dst_slot, c, kv],
            device_id=((chip_head(j), ctx), (head, next_ctx))[kv],
            device_id_type=MESH,
        )

    def all_copies(c):
        made = [own_onward(c), to_sibling(c, 0)]
        made += [own_across(c, j) for j in range(1, chips)]
        made += [to_sibling(c, slot_of(1, 0, 0))]
        for j in range(1, chips):
            made += [relayed(c, 0, j), relayed(c, 1, j)]
            made += [to_sibling(c, slot_of(0, j, 0)), to_sibling(c, slot_of(1, j, 0))]
        return made

    for c in range(pieces):
        for kv in range(2):
            local_kv(c, kv).start()
    for h in range(early * per_piece):
        local_q(h).start()

    barrier = pltpu.get_barrier_semaphore()
    pl.semaphore_signal(barrier, inc=1, device_id=(sibling_head, ctx), device_id_type=MESH)
    for j in range(1, chips):
        pl.semaphore_signal(barrier, inc=1, device_id=(chip_head(j), ctx), device_id_type=MESH)
    pl.semaphore_signal(barrier, inc=1, device_id=(head, next_ctx), device_id_type=MESH)
    pl.semaphore_signal(barrier, inc=1, device_id=(head, prev_ctx), device_id_type=MESH)

    bias_ref[...] = key_bias(order_ref, block, n_head, n_ctx)
    m_ref[...] = jnp.zeros(m_ref.shape, jnp.float32)
    l_ref[...] = jnp.ones(l_ref.shape, jnp.float32)

    pl.semaphore_wait(barrier, chips + 2)

    def send_own(c):
        for kv in range(2):
            local_kv(c, kv).wait()
        for j in range(1, chips):
            own_across(c, j).start()
        own_onward(c).start()
        to_sibling(c, 0).start()

    def first_hop(c):
        own_onward(c).wait_recv()
        for j in range(1, chips):
            relayed(c, 0, j).start()
        for j in range(1, chips):
            own_across(c, j).wait_recv()
            relayed(c, 1, j).start()
        to_sibling(c, slot_of(1, 0, 0)).start()
        for j in range(1, chips):
            to_sibling(c, slot_of(0, j, 0)).start()

    def second_hop(c):
        for j in range(1, chips):
            for kv in range(2):
                relayed(c, kv, j).wait_recv()
            to_sibling(c, slot_of(1, j, 0)).start()

    def last_hop(c):
        for p in range(2):
            for j in range(chips):
                to_sibling(c, slot_of(p, j, 0)).wait_recv()

    stat_lane = lax.broadcasted_iota(jnp.int32, (block, m_ref.shape[1]), 1)

    def attend(c, sub):
        h = c * per_piece + sub
        local_q(h).wait()
        k_h = kvearly[c, :, 0, :, sub * d : (sub + 1) * d].reshape(n_keys, d)
        v_h = kvearly[c, :, 1, :, sub * d : (sub + 1) * d].reshape(n_keys, d)

        def put(g, tile):
            start = pl.multiple_of(h * width + g * d, d)
            out_ref[:, pl.ds(start, d)] = tile

        attend_head(h, group, qbuf.at[h], k_h, v_h, bias_ref, m_ref, l_ref, stat_lane, put)

    for c in range(min(AHEAD, pieces)):
        send_own(c)

    half = (per_piece + 1) // 2
    for i in range(pieces + 1):
        if i < pieces:
            first_hop(i)
        if i + AHEAD < pieces:
            send_own(i + AHEAD)
        if i == pieces:
            second_hop(i - 1)
        if 0 <= i - 2 < early:
            for sub in range(half, per_piece):
                attend(i - 2, sub)
        if 0 < i < pieces:
            second_hop(i - 1)
        if i > 0:
            last_hop(i - 1)
        if 0 <= i - 1 < early:
            for sub in range(half if i < pieces else per_piece):
                attend(i - 1, sub)
    for c in range(pieces):
        for copy in all_copies(c):
            copy.wait_send()


def body(query, key, value, block_order):
    n_head = lax.axis_size("head")
    n_ctx = lax.axis_size("ctx")
    block, q_width = query.shape
    d = HEAD_DIMENSION
    kv_heads = key.shape[1] // d
    q_heads = q_width // d
    slots = 2 * n_head
    per_piece = math.gcd(HEADS_PER_PIECE, kv_heads)
    pieces = kv_heads // per_piece
    per_piece = math.gcd(HEADS_PER_PIECE, kv_heads)
    pieces = kv_heads // per_piece
    late = 1
    early = pieces - late
    width = q_width // kv_heads
    piece_shape = (slots, 2, block, per_piece * d)
    anywhere = pl.BlockSpec(memory_space=pltpu.HBM)
    vmem = pl.BlockSpec(memory_space=pltpu.VMEM)
    smem = pl.BlockSpec(memory_space=pltpu.SMEM)
    query, key, value, block_order = (
        pltpu.with_memory_space_constraint(x, pltpu.HBM) for x in (query, key, value, block_order)
    )
    early_rows, late_kv, stats, bias = pl.pallas_call(
        functools.partial(kernel, n_head, n_ctx),
        out_shape=(
            jax.ShapeDtypeStruct((block, early * per_piece * width), jnp.bfloat16),
            jax.ShapeDtypeStruct((late, *piece_shape), jnp.bfloat16),
            jax.ShapeDtypeStruct((2, block, q_heads), jnp.float32),
            jax.ShapeDtypeStruct((block, slots * block), jnp.float32),
        ),
        in_specs=[smem, anywhere, anywhere, anywhere],
        out_specs=(vmem, vmem, vmem, vmem),
        scratch_shapes=[
            pltpu.VMEM((early * per_piece, block, width), jnp.bfloat16),
            pltpu.VMEM((early, *piece_shape), jnp.bfloat16),
            pltpu.SemaphoreType.DMA((early * per_piece,)),
            pltpu.SemaphoreType.DMA((pieces, 2)),
            pltpu.SemaphoreType.DMA((slots, pieces, 2)),
            pltpu.SemaphoreType.DMA((slots, pieces, 2)),
        ],
        compiler_params=pltpu.CompilerParams(
            collective_id=0, has_side_effects=True, vmem_limit_bytes=VMEM_LIMIT
        ),
    )(block_order, query, key, value)
    return pl.pallas_call(
        functools.partial(finish_kernel, early),
        out_shape=(
            jax.ShapeDtypeStruct((block, q_width), jnp.bfloat16),
            jax.ShapeDtypeStruct((block, q_heads), jnp.float32),
        ),
        in_specs=[vmem, anywhere, vmem, vmem, vmem],
        out_specs=(anywhere, vmem),
        scratch_shapes=[
            pltpu.VMEM((late * per_piece, block, width), jnp.bfloat16),
            pltpu.VMEM((late * per_piece, block, width), jnp.bfloat16),
            pltpu.VMEM((block, q_heads), jnp.float32),
            pltpu.VMEM((block, q_heads), jnp.float32),
            pltpu.SemaphoreType.DMA((late * per_piece,)),
            pltpu.SemaphoreType.DMA((late * per_piece + 1,)),
        ],
        compiler_params=pltpu.CompilerParams(vmem_limit_bytes=VMEM_LIMIT),
    )(bias, query, late_kv, early_rows, stats)


def solution(mesh):
    placed = (P(("head", "ctx"), None), P(("head", "ctx"), None), P(("head", "ctx"), None), P())
    return jax.shard_map(
        body,
        mesh=mesh,
        in_specs=placed,
        out_specs=(P(("head", "ctx"), None), P(("head", "ctx"), None)),
        check_vma=False,
    )
```

time: 80.7 us -> 29.5 us (0.37)
  the two profiles are of different devices: /device:TPU:0 before, /device:TPU:1 now
where the time goes in v2:
time: 29.5 us; the launch traced here: 29.3 us
  Pallas kernels  28.7 us (97%)
  between operations  0.64 us (2%)
    pallas_call x1, Pallas kernels, body(): pl.pallas_call(functools.partial(kernel, n_head, n_ctx), out_shape=(jax.S...  21.8 us
    pallas_call x1, Pallas kernels, body(): pl.pallas_call(functools.partial(finish_kernel, early), out_shape=(jax.Sh...  6.82 us

profile of v2, /device:TPU:1, one launch (start us, length us, event | category | flops | bytes accessed | tf_op | source)
XLA Modules:
  0.0 29.3 jit_solution(16672575303909947100)
XLA Ops:
  0.6 21.8 %shard_map.59 = (bf16[64,8192]{1,0:T(8,128)(2,1)S(1)}, bf16[1,8,2,64,512]{4,3,2,1,0:T(8,128)(2,1)S(1)}, f32[2,64,128]{2,1,0:T(8,128)S(1)}, f32[64,512]{1,0:T(8,128)S(1)}) custom-call(s32[32]{0:T(128)} %order_ref.1, bf16[64,16384]{1,0:T(8,128)(2,1)} %q_hbm.3, bf16[64,1024]{1,0:T(8,128)(2,1)} %k_hbm.1, bf16[64,1024]{1,0:T(8,128)(2,1)} %v_hbm.1), custom_call_target="tpu_custom_call" | custom-call | tf_op jit(solution)/shard_map/pallas_call | solution.py:339
  22.5 6.8 %shard_map.60 = (bf16[64,16384]{1,0:T(8,128)(2,1)}, f32[64,128]{1,0:T(8,128)}) custom-call(f32[64,512]{1,0:T(8,128)S(1)} %get-tuple-element.6.bias_ref, bf16[64,16384]{1,0:T(8,128)(2,1)} %q_hbm.3, bf16[1,8,2,64,512]{4,3,2,1,0:T(8,128)(2,1)S(1)} %get-tuple-element.7.kv_ref, bf16[64,8192]{1,0:T(8,128)(2,1)S(1)} %get-tuple-element.8.early_ref, ...), custom_call_target="tpu_custom_call" | custom-call | tf_op jit(solution)/shard_map/pallas_call | solution.py:361

commit v3 on v2

--- a/solution.py
+++ b/solution.py
@@ -11,7 +11,7 @@
 HEAD_DIMENSION = 128
 MASKED = -1e30
 FLOOR = -10000.0
-GROUPS_PER_DOT = 4
+GROUPS_PER_DOT = 2
 HEADS_PER_PIECE = 4
 AHEAD = 2
 VMEM_LIMIT = 24 * 1024 * 1024

time: 29.5 us -> 28.9 us (0.980)
  the two profiles are of different devices: /device:TPU:1 before, /device:TPU:0 now
where the time goes in v3:
time: 28.9 us; the launch traced here: 28.4 us
  Pallas kernels  27.7 us (96%)
  between operations  0.64 us (2%)
    pallas_call x1, Pallas kernels, body(): pl.pallas_call(functools.partial(kernel, n_head, n_ctx), out_shape=(jax.S...  21.2 us
    pallas_call x1, Pallas kernels, body(): pl.pallas_call(functools.partial(finish_kernel, early), out_shape=(jax.Sh...  6.55 us

profile of v3, /device:TPU:0, one launch (start us, length us, event | category | flops | bytes accessed | tf_op | source)
XLA Modules:
  0.0 28.4 jit_solution(11141413358812711665)
XLA Ops:
  0.6 21.2 %shard_map.59 = (bf16[64,8192]{1,0:T(8,128)(2,1)S(1)}, bf16[1,8,2,64,512]{4,3,2,1,0:T(8,128)(2,1)S(1)}, f32[2,64,128]{2,1,0:T(8,128)S(1)}, f32[64,512]{1,0:T(8,128)S(1)}) custom-call(s32[32]{0:T(128)} %order_ref.1, bf16[64,16384]{1,0:T(8,128)(2,1)} %q_hbm.3, bf16[64,1024]{1,0:T(8,128)(2,1)} %k_hbm.1, bf16[64,1024]{1,0:T(8,128)(2,1)} %v_hbm.1), custom_call_target="tpu_custom_call" | custom-call | tf_op jit(solution)/shard_map/pallas_call | solution.py:339
  21.8 6.6 %shard_map.60 = (bf16[64,16384]{1,0:T(8,128)(2,1)}, f32[64,128]{1,0:T(8,128)}) custom-call(f32[64,512]{1,0:T(8,128)S(1)} %get-tuple-element.6.bias_ref, bf16[64,16384]{1,0:T(8,128)(2,1)} %q_hbm.3, bf16[1,8,2,64,512]{4,3,2,1,0:T(8,128)(2,1)S(1)} %get-tuple-element.7.kv_ref, bf16[64,8192]{1,0:T(8,128)(2,1)S(1)} %get-tuple-element.8.early_ref, ...), custom_call_target="tpu_custom_call" | custom-call | tf_op jit(solution)/shard_map/pallas_call | solution.py:361
